TPU v7x, 32 devices: a 4x2x2 block of a 4x4x8 slice. The times are simulated.
32 devices in a mesh: dp: 4 (over y, z), tp: 8 (over x, core).
Axes of the slice: x: 4, y: 2, z: 2, core: 2. Of those that a mesh axis runs over, the one named last changes fastest.
The devices are a block of a 4x4x8 slice.
Arguments:
- hidden: bfloat16 [1024, 4096], P('dp'), parts along dimension 0
- w_q: bfloat16 [4096, 4096], P(None, 'tp')
- w_k: bfloat16 [4096, 4096], P(None, 'tp')
- w_v: bfloat16 [4096, 4096], P(None, 'tp')
- w_o: bfloat16 [4096, 4096], P('tp')
- q_norm_w: float32 [4096], P('tp')
- k_norm_w: float32 [4096], P('tp')
- post_norm_w: float32 [4096], replicated
- k_cache: bfloat16 [1024, 32, 32, 128], P('dp', None, 'tp'), parts along dimension 0
- v_cache: bfloat16 [1024, 32, 32, 128], P('dp', None, 'tp'), parts along dimension 0
- positions: int32 [1024], P('dp'), parts along dimension 0
Outputs:
- output 1: bfloat16 [1024, 4096], P('dp'), parts along dimension 0
- output 2: bfloat16 [1024, 32, 32, 128], P('dp', None, 'tp'), parts along dimension 0
- output 3: bfloat16 [1024, 32, 32, 128], P('dp', None, 'tp'), parts along dimension 0
There are 4 independent parts. A program takes and returns all parts, laid end to end along the dimension named above; an argument that names none is the same for every part.
All inputs are finite; a program needn't handle non-finite values.
Results may differ from a plain program's by a relative error of at most 0.0120168.
Values are sent between devices in bfloat16 or wider.
A program may use at most 768 MiB of HBM per device.

v0:
```python
import jax
import jax.numpy as jnp
from jax import lax
from jax.sharding import PartitionSpec as P

NORM_EPS = 1e-6
ROPE_BASE = 500000.0


def apply_rope(heads_val, positions):
    head_dim = heads_val.shape[-1]
    half = head_dim // 2
    inv_freq = ROPE_BASE ** (-2.0 * jnp.arange(half, dtype=jnp.float32) / head_dim)
    angles = positions.astype(jnp.float32)[:, None, None] * inv_freq[None, None, :]
    cos_tab = jnp.cos(angles)
    sin_tab = jnp.sin(angles)
    wide = heads_val.astype(jnp.float32)
    first = wide[..., :half]
    second = wide[..., half:]
    return jnp.concatenate([first * cos_tab - second * sin_tab, second * cos_tab + first * sin_tab], axis=-1).astype(jnp.bfloat16)


def write_slot(cache, new_vals, positions):
    slot_ids = jnp.arange(cache.shape[1], dtype=jnp.int32)
    at_slot = (slot_ids[None, :] == positions[:, None])[:, :, None, None]
    return jnp.where(at_slot, new_vals[:, None], cache)


def attend(q_rot, k_new, v_new, positions):
    slot_ids = jnp.arange(k_new.shape[1], dtype=jnp.int32)
    scores = jnp.einsum('bhd,bshd->bhs', q_rot, k_new, preferred_element_type=jnp.float32) * k_new.shape[3] ** -0.5
    valid = (slot_ids[None, :] <= positions[:, None])[:, None, :]
    scores = jnp.where(valid, scores, -1e30)
    probs = jax.nn.softmax(scores, axis=-1).astype(jnp.bfloat16)
    return jnp.einsum('bhs,bshd->bhd', probs, v_new, preferred_element_type=jnp.float32).astype(jnp.bfloat16)


def solution(mesh):
    def local_step(hidden, w_q, w_k, w_v, w_o, q_norm_w, k_norm_w, post_norm_w, k_cache, v_cache, positions):
        n_rows, width = hidden.shape
        local_heads, head_dim = k_cache.shape[2], k_cache.shape[3]
        q_local = jnp.dot(hidden, w_q, preferred_element_type=jnp.float32).astype(jnp.bfloat16).astype(jnp.float32)
        k_local = jnp.dot(hidden, w_k, preferred_element_type=jnp.float32).astype(jnp.bfloat16).astype(jnp.float32)
        v_local = jnp.dot(hidden, w_v, preferred_element_type=jnp.float32).astype(jnp.bfloat16)
        energy = jnp.stack([jnp.sum(q_local * q_local, axis=-1), jnp.sum(k_local * k_local, axis=-1)])
        energy = lax.psum(energy, 'tp')
        inv_rms = lax.rsqrt(energy / width + NORM_EPS)
        q_normed = (q_local * inv_rms[0][:, None] * q_norm_w).astype(jnp.bfloat16).reshape(n_rows, local_heads, head_dim)
        k_normed = (k_local * inv_rms[1][:, None] * k_norm_w).astype(jnp.bfloat16).reshape(n_rows, local_heads, head_dim)
        q_rot = apply_rope(q_normed, positions)
        k_rot = apply_rope(k_normed, positions)
        k_new = write_slot(k_cache, k_rot, positions)
        v_new = write_slot(v_cache, v_local.reshape(n_rows, local_heads, head_dim), positions)
        attn = attend(q_rot, k_new, v_new, positions)
        proj_part = jnp.dot(attn.reshape(n_rows, local_heads * head_dim), w_o, preferred_element_type=jnp.float32).astype(jnp.bfloat16)
        a_out = lax.psum(proj_part, 'tp').astype(jnp.float32)
        inv_out = lax.rsqrt(jnp.mean(a_out * a_out, axis=-1, keepdims=True) + NORM_EPS)
        hidden_out = (hidden.astype(jnp.float32) + a_out * inv_out * post_norm_w).astype(jnp.bfloat16)
        return hidden_out, k_new, v_new

    cache_spec = P('dp', None, 'tp', None)
    return jax.shard_map(local_step, mesh=mesh, in_specs=(P('dp', None), P(None, 'tp'), P(None, 'tp'), P(None, 'tp'), P('tp', None), P('tp'), P('tp'), P(None), cache_spec, cache_spec, P('dp')), out_specs=(P('dp', None), cache_spec, cache_spec), check_vma=False)
```

profile of v0, /device:TPU:81, one launch (start us, length us, event | category | flops | bytes accessed | tf_op | source)
XLA Modules:
  0.0 139.5 jit_solution(4069633255113001987)
XLA Ops:
  7.2 0.0 copy-start.1
  7.2 0.1 all-reduce.2.cloned.1.call-start
  7.3 0.8 convert_element_type.69
  8.1 0.8 iota_compare_fusion.1
  8.9 0.1 copy.14
  9.0 4.1 %convolution_convert_fusion.1 = bf16[256,512]{1,0:T(8,128)(2,1)S(1)} fusion(bf16[256,4096]{1,0:T(8,128)(2,1)} %param.11, bf16[4096,512]{1,0:T(8,128)(2,1)} %param.14), kind=kOutput, calls=%fused_computation.15 | convolution fusion | flops 1073872896 | bytes 6553600 | tf_op jit(solution)/shard_map/dot_general | solution.py:44
  13.0 0.1 broadcast_in_dim.62
  13.1 0.0 copy-done.1
  13.1 0.0 copy-start.6
  13.1 3.7 %multiply_reduce_fusion.1 = (f32[256]{0:T(256)S(1)}, f32[256,512]{1,0:T(8,128)S(1)}) fusion(bf16[256,4096]{1,0:T(8,128)(2,1)S(1)} %copy-done.1, bf16[4096,512]{1,0:T(8,128)(2,1)} %param.12), kind=kOutput, calls=%fused_computation.33 | convolution fusion | flops 1074265856 | bytes 6816768 | tf_op jit(solution)/shard_map/dot_general | solution.py:42
  16.8 0.0 copy-done.6
  16.8 0.0 copy-start.4
  16.8 0.0 copy-start.5
  16.8 1.4 multiply_reduce_fusion
  18.2 14.0 %psum.14 = f32[2,256]{1,0:T(2,128)S(1)} all-reduce(f32[2,256]{1,0:T(2,128)S(1)} %pad_maximum_fusion.1), channel_id=1, replica_groups=mesh['dp'=4,'tp'=8] {'tp'}, use_global_device_ids=true, to_apply=%region_2.0 | all-reduce | flops 512 | bytes 4096 | tf_op jit(solution)/shard_map/psum | solution.py:46
  32.3 0.0 copy-done.4
  32.3 0.1 fusion.18
  32.4 0.2 reshape.142
  32.6 0.0 copy-done.5
  32.6 0.1 fusion.19
  32.7 0.2 reshape.143
  32.9 0.5 multiply_cosine_fusion
  33.4 0.8 subtract_convert_fusion.1
  34.2 0.4 maximum_bitcast_fusion
  34.6 0.4 pad_maximum_fusion
  35.0 13.9 %broadcast_select_fusion = (bf16[256,32,4,128]{3,2,1,0:T(4,128)(2,1)}, bf16[256,32,4,128]{3,2,1,0:T(4,128)(2,1)S(1)}) fusion(bf16[256,32,4,128]{3,2,1,0:T(4,128)(2,1)} %param.20, pred[256,32]{1,0:T(8,128)(4,1)S(1)} %get-tuple-element.16, bf16[256,4,128]{2,1,0:T(4,128)(2,1)S(1)} %broadcast_in_dim.62, bf16[256,32,4,128]{3,2,1,0:T(4,128)(2,1)} %param.19, ...), kind=kLoop, calls=%fused_computation.6 | loop fusion | flops 8388608 | bytes 34086912 | tf_op jit(solution)/shard_map/jit(_where)/select_n | solution.py:26
  48.9 0.0 copy-start
  48.9 3.4 %copy-done = bf16[256,32,4,128]{3,2,1,0:T(4,128)(2,1)} copy-done((bf16[256,32,4,128]{3,2,1,0:T(4,128)(2,1)}, bf16[256,32,4,128]{3,2,1,0:T(4,128)(2,1)S(1)}, u32[]{:S(2)}) %copy-start) | copy-done | bytes 8388632
  52.3 4.5 %fusion.4 = f32[256,4,1,32]{3,2,1,0:T(1,128)S(1)} fusion(bf16[256,32,4,128]{3,2,1,0:T(4,128)(2,1)S(1)} %get-tuple-element.10, bf16[256,4,128,1]{2,1,0,3:T(4,128)(2,1)S(1)} %maximum_bitcast_fusion), kind=kOutput, calls=%fused_computation.4 | convolution fusion | flops 8388608 | bytes 8781824 | tf_op jit(solution)/shard_map/bhd,bshd->bhs/dot_general | solution.py:31
  56.8 0.4 copy.17
  57.2 0.1 fusion.16
  57.3 0.4 copy.18
  57.7 0.0 copy-start.7
  57.7 5.8 %fusion.2 = f32[256,4,1,128]{3,2,1,0:T(1,128)S(1)} fusion(bf16[256,4,32,1]{2,3,1,0:T(2,128)(2,1)S(1)} %copy.18, bf16[256,32,4,128]{3,2,1,0:T(4,128)(2,1)} %get-tuple-element.9), kind=kOutput, calls=%fused_computation.2 | convolution fusion | flops 8388608 | bytes 8978432 | tf_op jit(solution)/shard_map/bhs,bshd->bhd/dot_general | solution.py:35
  63.5 0.1 convert_element_type.75
  63.7 0.0 copy-done.7
  63.7 2.6 %convolution_convert_fusion = bf16[256,4096]{1,0:T(8,128)(2,1)} fusion(bf16[512,4096]{1,0:T(8,128)(2,1)S(1)} %copy-done.7, bf16[32,8,4,128]{3,2,1,0:T(4,128)(2,1)S(1)} %bitcast.32), kind=kOutput, calls=%fused_computation.10 | convolution fusion | flops 1074790400 | bytes 6553600 | tf_op jit(solution)/shard_map/dot_general | solution.py:55
  66.3 0.0 copy-start.2
  66.3 0.0 copy-start.3
  66.3 0.1 all-reduce.2.cloned.1.call-update
  66.3 60.2 %all-reduce.2.cloned.1.call-done = bf16[256,4096]{1,0:T(8,128)(2,1)} async-done(((bf16[256,4096]{1,0:T(8,128)(2,1)}), bf16[256,4096]{1,0:T(8,128)(2,1)}) %all-reduce.2.cloned.1.call-update) | async-done | bytes 2097168 | tf_op jit(solution)/shard_map/psum | solution.py:56
  126.5 2.1 %fusion.6 = f32[256]{0:T(256)S(1)} fusion(bf16[256,4096]{1,0:T(8,128)(2,1)} %all-reduce.2.cloned.1.call-done), kind=kLoop, calls=%fused_computation.11 | loop fusion | flops 3145472 | bytes 2098176 | tf_op jit(solution)/shard_map/reduce_sum | solution.py:57
  128.6 0.0 copy-done.2
  128.6 0.0 copy-done.3
  128.6 4.0 %fusion.9 = bf16[256,4096]{1,0:T(8,128)(2,1)} fusion(bf16[256,4096]{1,0:T(8,128)(2,1)} %all-reduce.2.cloned.1.call-done, bf16[256,4096]{1,0:T(8,128)(2,1)S(1)} %copy-done.2, f32[4096]{0:T(1024)S(1)} %copy-done.3, f32[256]{0:T(256)S(1)} %add_rsqrt_fusion.1), kind=kLoop, calls=%fused_computation.14 | loop fusion | flops 6291456 | bytes 6308864 | tf_op jit(solution)/shard_map/convert_element_type | solution.py:58
  (5 shorter events, 0.0 us)
Async XLA Ops:
  7.2 5.9 %copy-start.1 = (bf16[256,4096]{1,0:T(8,128)(2,1)S(1)}, bf16[256,4096]{1,0:T(8,128)(2,1)}, u32[]{:S(2)}) copy-start(bf16[256,4096]{1,0:T(8,128)(2,1)} %param.11) | copy-start | bytes 6291460
  7.2 119.3 %all-reduce.2.cloned.1.call-start = ((), (), s32[]{:S(2)}) async-start(), calls=%async_computation | async-start | bytes 4194304 | tf_op jit(solution)/shard_map/psum | solution.py:56
  13.1 3.7 %copy-start.6 = (bf16[4096,512]{1,0:T(8,128)(2,1)S(1)}, bf16[4096,512]{1,0:T(8,128)(2,1)}, u32[]{:S(2)}) copy-start(bf16[4096,512]{1,0:T(8,128)(2,1)} %param.13) | copy-start | bytes 12582916
  16.8 15.5 %copy-start.4 = (f32[512]{0:T(512)S(1)}, f32[512]{0:T(512)}, u32[]{:S(2)}) copy-start(f32[512]{0:T(512)} %param.16) | copy-start | bytes 6148
  16.8 15.8 %copy-start.5 = (f32[512]{0:T(512)S(1)}, f32[512]{0:T(512)}, u32[]{:S(2)}) copy-start(f32[512]{0:T(512)} %param.17) | copy-start | bytes 6148
  48.9 3.4 %copy-start = (bf16[256,32,4,128]{3,2,1,0:T(4,128)(2,1)}, bf16[256,32,4,128]{3,2,1,0:T(4,128)(2,1)S(1)}, u32[]{:S(2)}) copy-start(bf16[256,32,4,128]{3,2,1,0:T(4,128)(2,1)S(1)} %get-tuple-element.10) | copy-start | bytes 25165828
  57.7 5.9 %copy-start.7 = (bf16[512,4096]{1,0:T(8,128)(2,1)S(1)}, bf16[512,4096]{1,0:T(8,128)(2,1)}, u32[]{:S(2)}) copy-start(bf16[512,4096]{1,0:T(8,128)(2,1)} %param.15) | copy-start | bytes 12582916
  66.3 62.4 %copy-start.2 = (bf16[256,4096]{1,0:T(8,128)(2,1)S(1)}, bf16[256,4096]{1,0:T(8,128)(2,1)}, u32[]{:S(2)}) copy-start(bf16[256,4096]{1,0:T(8,128)(2,1)} %param.11) | copy-start | bytes 6291460
  66.3 62.4 %copy-start.3 = (f32[4096]{0:T(1024)S(1)}, f32[4096]{0:T(1024)}, u32[]{:S(2)}) copy-start(f32[4096]{0:T(1024)} %param.18) | copy-start | bytes 49156
Sparse Core Ops, SparseCore 0:
  66.5 60.0 all-reduce.1
where the time goes:
time: 140 us; the launch traced here: 139 us
  waiting for transfers between devices  60.3 us (43%)
  other arithmetic  24 us (17%)
  matrix products  22 us (16%)
  between operations  14.3 us (10%)
  blocking collectives  14 us (10%)
  local copies, waits for them, and re-layouts  4.79 us (3%)
    psum x1, waiting for transfers between devices, local_step(): a_out = lax.psum(proj_part, 'tp').astype(jnp.float32)  60.2 us
    psum x1, blocking collectives, local_step(): energy = lax.psum(energy, 'tp')  14 us
    select_n x1, other arithmetic, write_slot(): return jnp.where(at_slot, new_vals[:, None], cache)  13.9 us
    dot_general x1, matrix products, attend(): jnp.einsum('bhs,bshd->bhd', probs, v_new, preferred_element_type=jnp.floa...  5.8 us
    dot_general x1, matrix products, attend(): jnp.einsum('bhd,bshd->bhs', q_rot, k_new, preferred_element_type=jnp.floa...  4.52 us
    dot_general x1, matrix products, local_step(): jnp.dot(hidden, w_v, preferred_element_type=jnp.float32)  4.06 us
    convert_element_type x1, other arithmetic, local_step(): (hidden.astype(jnp.float32) + a_out * inv_out * post_norm_w).astype(jnp.b...  3.97 us
    dot_general x1, matrix products, local_step(): jnp.dot(hidden, w_q, preferred_element_type=jnp.float32)  3.66 us
  transfers between devices with their start and end apart: 1, of which 1 were waited for; matrix products, arithmetic and copies ran while one was open for 0% of the time, Pallas kernels for 0%

commit v1 on v0

v1 whole, which is shorter than its diff:
```python
import functools

import jax
import jax.numpy as jnp
from jax import lax
from jax.experimental import pallas as pl
from jax.experimental.pallas import tpu as pltpu
from jax.sharding import PartitionSpec as P

NORM_EPS = 1e-6
ROPE_BASE = 500000.0
MESH = pl.DeviceIdType.MESH
LANES = 128
F32 = jnp.float32
BF16 = jnp.bfloat16
K_CHUNKS = 4
GROUP = 16


def column(row_vals, count):
    blocks = []
    for i in range(count):
        block = jnp.broadcast_to(row_vals[i:i + 1, :], (LANES, LANES))
        blocks.append(block.T)
    return jnp.concatenate(blocks, axis=0) if count > 1 else blocks[0]


def project_kernel(n_tp, hidden, w_q, w_k, w_v, q_gain, k_gain, pos, freq, sign, q_out, k_out, v_out,
                   hbuf, wbuf, acc, cos_tab, sin_tab, e_send, e_recv, h_sems, w_sems, send_sems, recv_sems):
    me = lax.axis_index('tp')
    n_rows, width = hidden.shape
    cols = w_q.shape[1]
    heads = cols // LANES
    depth = width // K_CHUNKS

    def h_copy(c):
        part = pl.ds(c * depth, depth)
        return pltpu.make_async_copy(hidden.at[:, part], hbuf.at[c], h_sems.at[c])

    def w_copy(w, i, c):
        part = pl.ds(c * depth, depth)
        return pltpu.make_async_copy(w.at[part, :], wbuf.at[i * K_CHUNKS + c], w_sems.at[i * K_CHUNKS + c])

    for i, w in enumerate((w_q, w_k, w_v)):
        for c in range(K_CHUNKS):
            if i == 0:
                h_copy(c).start()
            w_copy(w, i, c).start()
    barrier = pltpu.get_barrier_semaphore()
    for d in range(1, n_tp):
        pl.semaphore_signal(barrier, inc=1, device_id={'tp': lax.rem(me + d, n_tp)}, device_id_type=MESH)

    angle = column(pos[...].astype(F32), n_rows // LANES) * freq[...]
    cos_tab[...] = jnp.cos(angle)
    sin_tab[...] = jnp.sin(angle) * sign[...]

    def matmul(i, w):
        def chunk(c, carry):
            @pl.when(i * K_CHUNKS + c < K_CHUNKS)
            def _():
                h_copy(c).wait()
            w_copy(w, i, c).wait()
            part = jnp.dot(hbuf[c], wbuf[i * K_CHUNKS + c], preferred_element_type=F32)
            @pl.when(c == 0)
            def _():
                acc[i] = part
            @pl.when(c > 0)
            def _():
                acc[i] = acc[i] + part
            return carry
        lax.fori_loop(0, K_CHUNKS, chunk, 0)

    matmul(0, w_q)
    matmul(1, w_k)
    lane = lax.broadcasted_iota(jnp.int32, (n_rows, LANES), 1)
    sums = []
    for i in range(2):
        wide = acc[i].astype(BF16).astype(F32)
        sums.append(jnp.sum(wide * wide, axis=1, keepdims=True))
    both = jnp.where(lane < 4, sums[0], sums[1])
    e_send[...] = both.T[0:8, :]
    pl.semaphore_wait(barrier, n_tp - 1)
    copies = []
    for d in range(1, n_tp):
        copies.append(pltpu.make_async_remote_copy(
            src_ref=e_send, dst_ref=e_recv.at[d - 1], send_sem=send_sems.at[d - 1], recv_sem=recv_sems.at[d - 1],
            device_id={'tp': lax.rem(me + d, n_tp)}, device_id_type=MESH))
        copies[-1].start()
    matmul(2, w_v)
    for h in range(heads):
        v_out[h] = acc[2, :, h * LANES:(h + 1) * LANES].astype(BF16)
    total = e_send[...]
    for d in range(1, n_tp):
        copies[d - 1].wait_recv()
        total = total + e_recv[d - 1]
    inv = lax.rsqrt(total / width + NORM_EPS)
    inv_cols = jnp.concatenate([inv] * (LANES // 8), axis=0).T
    cos_val = cos_tab[...]
    sin_val = sin_tab[...]
    for i, (gain, out) in enumerate(((q_gain, q_out), (k_gain, k_out))):
        inv_col = inv_cols[:, 4 * i:4 * i + 1]
        for h in range(heads):
            part = slice(h * LANES, (h + 1) * LANES)
            wide = acc[i, :, part].astype(BF16).astype(F32)
            normed = (wide * inv_col * gain[:, part]).astype(BF16).astype(F32)
            out[h] = (normed * cos_val + pltpu.roll(normed, LANES // 2, 1) * sin_val).astype(BF16)
    for copy in copies:
        copy.wait_send()


def attend_kernel(slots, heads, pos_smem, pos, q, k, v, k_cache, v_cache, k_new, v_new, o,
                  kbuf, vbuf, k_rows, v_rows, pos_col, in_sems, out_sems):
    n_rows = q.shape[1]
    span = slots * heads
    n_groups = n_rows // GROUP
    block = GROUP * span

    def in_copy(i, g):
        src, dst = ((k_cache, kbuf), (v_cache, vbuf))[i]
        part = pl.ds(g * block, block)
        return pltpu.make_async_copy(src.at[part, :], dst.at[part, :], in_sems.at[i, g])

    def out_copy(i, g):
        src, dst = ((kbuf, k_new), (vbuf, v_new))[i]
        part = pl.ds(g * block, block)
        return pltpu.make_async_copy(src.at[part, :], dst.at[part, :], out_sems.at[i, g])

    for g in range(n_groups):
        in_copy(0, g).start()
        in_copy(1, g).start()
    pos_col[...] = column(pos[...].astype(F32), n_rows // LANES)
    for src, dst in ((k, k_rows), (v, v_rows)):
        for r in range(8):
            dst[pl.ds(r, n_rows, stride=8), :] = src[r % heads].astype(F32)

    m_rows = heads * GROUP
    row_b = lax.broadcasted_iota(jnp.int32, (m_rows, LANES), 0) % GROUP
    row_h = lax.broadcasted_iota(jnp.int32, (m_rows, LANES), 0) // GROUP
    lane = lax.broadcasted_iota(jnp.int32, (m_rows, LANES), 1)
    own_head = (lane % heads) == row_h
    lane_slot = (lane // heads).astype(F32)
    tile_slot = lax.broadcasted_iota(jnp.int32, (16, LANES), 0) // heads
    per_tile = 16 // heads
    scale = LANES ** -0.5

    def group(g, carry):
        in_copy(0, g).wait()
        in_copy(1, g).wait()
        for b in range(GROUP):
            row = g * GROUP + b
            p = pos_smem[row]
            at = pl.multiple_of(row * span + (p // per_tile) * 16, 16)
            hit = tile_slot == p % per_tile
            for buf, rows in ((kbuf, k_rows), (vbuf, v_rows)):
                new = rows[pl.ds(pl.multiple_of(row * 8, 8), 8), :]
                new = jnp.concatenate([new, new], axis=0)
                old = buf[pl.ds(at, 16), :].astype(F32)
                buf[pl.ds(at, 16), :] = jnp.where(hit, new, old).astype(BF16)
        here = pl.ds(pl.multiple_of(g * block, block), block)
        rows_here = pl.ds(pl.multiple_of(g * GROUP, GROUP), GROUP)
        lhs = q[:, rows_here, :].reshape(m_rows, LANES)
        scores = lax.dot_general(lhs, kbuf[here, :], (((1,), (1,)), ((), ())), preferred_element_type=F32)
        mine = scores[:, 0:span]
        for b in range(1, GROUP):
            mine = jnp.where(row_b == b, scores[:, b * span:(b + 1) * span], mine)
        limit = pos_col[rows_here, :]
        limit = jnp.concatenate([limit] * heads, axis=0)
        mine = jnp.where(own_head & (lane_slot <= limit), mine * scale, -1e30)
        top = jnp.max(mine, axis=1, keepdims=True)
        e = jnp.exp(mine - top)
        probs = e / jnp.sum(e, axis=1, keepdims=True)
        wide = jnp.concatenate([jnp.where(row_b == b, probs, 0.0).astype(BF16) for b in range(GROUP)], axis=1)
        mixed = jnp.dot(wide, vbuf[here, :], preferred_element_type=F32).astype(BF16)
        for h in range(heads):
            o[rows_here, h * LANES:(h + 1) * LANES] = mixed[h * GROUP:(h + 1) * GROUP, :]
        out_copy(0, g).start()
        out_copy(1, g).start()
        return carry

    lax.fori_loop(0, n_groups, group, 0)
    for g in range(n_groups):
        out_copy(0, g).wait()
        out_copy(1, g).wait()


def combine_kernel(n_tp, n_chunks, o, w_o, hidden, gain, out,
                   wbuf, obuf, sib_send, sib_recv, own, ring_send, far_recv, near_send, near_recv,
                   w_sems, h_sem, hbuf, sib_s, sib_r, far_s, far_r, imm_s, imm_r, dep_s, dep_r, ag_s, ag_r):
    me = lax.axis_index('tp')
    chips = n_tp // 2
    x, c = me // 2, me % 2
    n_rows, width = hidden.shape
    half = width // 2
    blk = n_rows // n_chunks // n_tp
    side_rows = blk * chips
    chunk_rows = n_rows // n_chunks
    tile = 512
    n_tiles = width // tile
    right_x, left_x, far_x = lax.rem(x + 1, chips), lax.rem(x + chips - 1, chips), lax.rem(x + 2, chips)
    sib = {'tp': 2 * x + 1 - c}
    right = {'tp': 2 * right_x + c}
    left = {'tp': 2 * left_x + c}

    def w_copy(n):
        part = pl.ds(n * tile, tile)
        return pltpu.make_async_copy(w_o.at[:, part], wbuf.at[n], w_sems.at[n])

    for n in range(n_tiles):
        w_copy(n).start()
    barrier = pltpu.get_barrier_semaphore()
    for peer in (sib, right, left):
        pl.semaphore_signal(barrier, inc=1, device_id=peer, device_id_type=MESH)

    def remote(src, dst, s, r, peer):
        return pltpu.make_async_remote_copy(src_ref=src, dst_ref=dst, send_sem=s, recv_sem=r, device_id=peer, device_id_type=MESH)

    def block_of(which):
        return pl.ds(pl.multiple_of(which * blk, blk), blk)

    def out_rows(j, core, which):
        return pl.ds(pl.multiple_of(j * chunk_rows + core * side_rows + which * blk, blk), blk)

    def sib_copy(j, s):
        return remote(sib_send.at[j, s], sib_recv.at[j, s], sib_s.at[j, s], sib_r.at[j, s], sib)

    fwd = (right, left)

    def far_copy(j, s):
        return remote(ring_send.at[j, s], far_recv.at[j, s], far_s.at[j, s], far_r.at[j, s], fwd[s])

    def imm_copy(j, s):
        return remote(near_send.at[j, s, 1 - s], near_recv.at[j, s, 1 - s], imm_s.at[j, s], imm_r.at[j, s], fwd[s])

    def dep_copy(j, s):
        return remote(near_send.at[j, s, s], near_recv.at[j, s, s], dep_s.at[j, s], dep_r.at[j, s], fwd[s])

    fwd_x = (right_x, left_x)
    back_x = (left_x, right_x)

    def ag_copy(j, kind):
        if kind < 2:
            rows, part, peer = out_rows(j, c, x), slice(None), fwd[kind]
        elif kind < 4:
            s = kind - 2
            rows, part, peer = out_rows(j, c, back_x[s]), pl.ds(s * half, half), fwd[s]
        elif kind == 4:
            rows, part, peer = out_rows(j, c, x), slice(None), sib
        elif kind < 7:
            rows, part, peer = out_rows(j, c, back_x[kind - 5]), slice(None), sib
        else:
            rows, part, peer = out_rows(j, c, far_x), pl.ds((kind - 7) * half, half), sib
        ref = out.at[rows, part]
        return remote(ref, ref, ag_s.at[j, kind], ag_r.at[j, kind], peer)

    h_copies = []
    for j in range(n_chunks):
        rows = out_rows(j, c, x)
        h_copies.append(pltpu.make_async_copy(hidden.at[rows, :], hbuf.at[j], h_sem.at[j]))
        h_copies[-1].start()

    def project(j):
        mine = pl.ds(pl.multiple_of(j * chunk_rows + c * side_rows, side_rows), side_rows)
        theirs = pl.ds(pl.multiple_of(j * chunk_rows + (1 - c) * side_rows, side_rows), side_rows)
        obuf[0:side_rows, :] = o[theirs, :]
        obuf[side_rows:, :] = o[mine, :]
        for s in range(2):
            def tiles(n, carry):
                idx = s * (n_tiles // 2) + n
                if j == 0:
                    w_copy(idx).wait()
                part = jnp.dot(obuf[...], wbuf[idx], preferred_element_type=F32)
                at = pl.ds(pl.multiple_of(n * tile, tile), tile)
                sib_send[j, s, :, at] = part[0:side_rows].astype(BF16)
                own[j, s, :, at] = part[side_rows:]
                return carry
            lax.fori_loop(0, n_tiles // 2, tiles, 0)
            if j == 0 and s == 0:
                pl.semaphore_wait(barrier, 3)
            sib_copy(j, s).start()

    def chip_sum(j, s, which):
        rows = block_of(which)
        return own[j, s, rows, :] + sib_recv[j, s, rows, :].astype(F32)

    def scatter(j):
        for s in range(2):
            sib_copy(j, s).wait_recv()
            ring_send[j, s] = chip_sum(j, s, far_x).astype(BF16)
            far_copy(j, s).start()
        for s in range(2):
            near_send[j, s, 1 - s] = chip_sum(j, 1 - s, fwd_x[s]).astype(BF16)
            imm_copy(j, s).start()

    def relay(j):
        for s in range(2):
            far_copy(j, s).wait_recv()
            near_send[j, s, s] = (chip_sum(j, s, fwd_x[s]) + far_recv[j, s].astype(F32)).astype(BF16)
            dep_copy(j, s).start()

    def finish(j):
        parts = []
        h_copies[j].wait()
        for s in range(2):
            imm_copy(j, s).wait_recv()
            dep_copy(j, s).wait_recv()
        energy = 0.0
        for s in range(2):
            a = chip_sum(j, s, x) + near_recv[j, 0, s].astype(F32) + near_recv[j, 1, s].astype(F32)
            parts.append(a)
            energy = energy + jnp.sum(a * a, axis=1, keepdims=True)
        inv = lax.rsqrt(energy / width + NORM_EPS)
        rows = out_rows(j, c, x)
        for s in range(2):
            part = slice(s * half, (s + 1) * half)
            out[rows, part] = (hbuf[j, :, part].astype(F32) + parts[s] * inv * gain[:, part]).astype(BF16)

    def gather_first(j):
        for kind in (0, 1, 4):
            ag_copy(j, kind).start()

    def gather_relay(j):
        for s in range(2):
            ag_copy(j, s).wait_recv()
            ag_copy(j, 2 + s).start()
            ag_copy(j, 5 + s).start()

    def gather_last(j):
        for s in range(2):
            ag_copy(j, 2 + s).wait_recv()
            ag_copy(j, 7 + s).start()

    project(0)
    scatter(0)
    project(1)
    relay(0)
    scatter(1)
    finish(0)
    gather_first(0)
    relay(1)
    gather_relay(0)
    finish(1)
    gather_first(1)
    gather_last(0)
    gather_relay(1)
    gather_last(1)
    for j in range(n_chunks):
        for kind in range(4, 9):
            ag_copy(j, kind).wait_recv()
        for s in range(2):
            sib_copy(j, s).wait_send()
            far_copy(j, s).wait_send()
            imm_copy(j, s).wait_send()
            dep_copy(j, s).wait_send()
        for kind in range(9):
            ag_copy(j, kind).wait_send()


VMEM = pl.BlockSpec(memory_space=pltpu.VMEM)
SMEM = pl.BlockSpec(memory_space=pltpu.SMEM)
ANY = pl.BlockSpec(memory_space=pl.ANY)
DMA = pltpu.SemaphoreType.DMA


def solution(mesh):
    n_tp = mesh.shape['tp']
    n_chunks = 2

    def local_step(hidden, w_q, w_k, w_v, w_o, q_norm_w, k_norm_w, post_norm_w, k_cache, v_cache, positions):
        n_rows, width = hidden.shape
        slots, heads, head_dim = k_cache.shape[1:]
        cols = heads * head_dim
        depth = width // K_CHUNKS
        half = head_dim // 2
        inv_freq = ROPE_BASE ** (-2.0 * jnp.arange(half, dtype=F32) / head_dim)
        freq = jnp.concatenate([inv_freq, inv_freq])[None, :]
        sign = jnp.concatenate([-jnp.ones((half,), F32), jnp.ones((half,), F32)])[None, :]
        pos = positions.reshape(n_rows // LANES, LANES)
        by_head = jax.ShapeDtypeStruct((heads, n_rows, head_dim), BF16)
        q, k, v = pl.pallas_call(
            functools.partial(project_kernel, n_tp),
            out_shape=(by_head, by_head, by_head),
            in_specs=[ANY] * 4 + [VMEM] * 5,
            out_specs=(VMEM,) * 3,
            scratch_shapes=[
                pltpu.VMEM((K_CHUNKS, n_rows, depth), BF16),
                pltpu.VMEM((3 * K_CHUNKS, depth, cols), BF16),
                pltpu.VMEM((3, n_rows, cols), F32),
                pltpu.VMEM((n_rows, LANES), F32),
                pltpu.VMEM((n_rows, LANES), F32),
                pltpu.VMEM((8, n_rows), F32),
                pltpu.VMEM((n_tp - 1, 8, n_rows), F32),
                DMA((K_CHUNKS,)),
                DMA((3 * K_CHUNKS,)),
                DMA((n_tp - 1,)),
                DMA((n_tp - 1,)),
            ],
            compiler_params=pltpu.CompilerParams(collective_id=0, has_side_effects=True, vmem_limit_bytes=60 * 2**20),
            name='project',
        )(hidden, w_q, w_k, w_v, q_norm_w[None, :], k_norm_w[None, :], pos, freq, sign)

        flat = (n_rows * slots * heads, head_dim)
        n_groups = n_rows // GROUP
        k_new, v_new, o = pl.pallas_call(
            functools.partial(attend_kernel, slots, heads),
            out_shape=(jax.ShapeDtypeStruct(flat, BF16), jax.ShapeDtypeStruct(flat, BF16), jax.ShapeDtypeStruct((n_rows, cols), BF16)),
            in_specs=[SMEM] + [VMEM] * 4 + [ANY] * 2,
            out_specs=(ANY, ANY, VMEM),
            scratch_shapes=[
                pltpu.VMEM(flat, BF16),
                pltpu.VMEM(flat, BF16),
                pltpu.VMEM((n_rows * 8, head_dim), F32),
                pltpu.VMEM((n_rows * 8, head_dim), F32),
                pltpu.VMEM((n_rows, LANES), F32),
                DMA((2, n_groups)),
                DMA((2, n_groups)),
            ],
            compiler_params=pltpu.CompilerParams(vmem_limit_bytes=60 * 2**20),
            name='attend',
        )(positions, pos, q, k, v, k_cache.reshape(flat), v_cache.reshape(flat))

        blk = n_rows // n_chunks // n_tp
        side_rows = blk * (n_tp // 2)
        wide = width // 2
        out = pl.pallas_call(
            functools.partial(combine_kernel, n_tp, n_chunks),
            out_shape=jax.ShapeDtypeStruct((n_rows, width), BF16),
            in_specs=[VMEM, ANY, ANY, VMEM],
            out_specs=VMEM,
            scratch_shapes=[
                pltpu.VMEM((width // 512, cols, 512), BF16),
                pltpu.VMEM((2 * side_rows, cols), BF16),
                pltpu.VMEM((n_chunks, 2, side_rows, wide), BF16),
                pltpu.VMEM((n_chunks, 2, side_rows, wide), BF16),
                pltpu.VMEM((n_chunks, 2, side_rows, wide), F32),
                pltpu.VMEM((n_chunks, 2, blk, wide), BF16),
                pltpu.VMEM((n_chunks, 2, blk, wide), BF16),
                pltpu.VMEM((n_chunks, 2, 2, blk, wide), BF16),
                pltpu.VMEM((n_chunks, 2, 2, blk, wide), BF16),
                DMA((width // 512,)),
                DMA((n_chunks,)),
                pltpu.VMEM((n_chunks, blk, width), BF16),
            ] + [DMA((n_chunks, 2))] * 8 + [DMA((n_chunks, 9))] * 2,
            compiler_params=pltpu.CompilerParams(collective_id=1, has_side_effects=True, vmem_limit_bytes=60 * 2**20),
            name='combine',
        )(o, w_o, hidden, post_norm_w[None, :])
        return out, k_new.reshape(k_cache.shape), v_new.reshape(v_cache.shape)

    cache_spec = P('dp', None, 'tp', None)
    return jax.shard_map(local_step, mesh=mesh, in_specs=(P('dp', None), P(None, 'tp'), P(None, 'tp'), P(None, 'tp'), P('tp', None), P('tp'), P('tp'), P(None), cache_spec, cache_spec, P('dp')), out_specs=(P('dp', None), cache_spec, cache_spec), check_vma=False)
```

time: 140 us -> 68.8 us (0.49)
  Pallas kernels: 0 us -> 64.2 us
  waiting for transfers between devices: 60.3 us -> 0 us
  other arithmetic: 24 us -> 0.6 us
  matrix products: 22 us -> 0 us
  blocking collectives: 14 us -> 0 us
  between operations: 14.3 us -> 0.66 us
  local copies, waits for them, and re-layouts: 4.79 us -> 3.13 us
    pallas_call x0 -> x3, Pallas kernels: none -> 64.2 us  [the longest x1 32 us: local_step(): pl.pallas_call(functools.partial(combine_kernel, n_tp, n_chunks), out_sha...]
    psum x1 -> x0, waiting for transfers between devices: 60.2 us -> none  [local_step(): a_out = lax.psum(proj_part, 'tp').astype(jnp.float32)]
    dot_general x6 -> x0, matrix products: 22 us -> none  [the longest x1 5.8 us: attend(): jnp.einsum('bhs,bshd->bhd', probs, v_new, preferred_element_type=jnp.floa...]
    psum x1 -> x0, blocking collectives: 14 us -> none  [local_step(): energy = lax.psum(energy, 'tp')]
    select_n x1 -> x0, other arithmetic: 13.9 us -> none  [write_slot(): return jnp.where(at_slot, new_vals[:, None], cache)]
    convert_element_type x5 -> x0, other arithmetic: 5.11 us -> none  [the longest x1 3.97 us: local_step(): (hidden.astype(jnp.float32) + a_out * inv_out * post_norm_w).astype(jnp.b...]
    reduce_sum x1 -> x0, other arithmetic: 2.08 us -> none  [local_step(): jnp.mean(a_out * a_out, axis=-1, keepdims=True) + NORM_EPS]
    unnamed x16 -> x1, local copies, waits for them, and re-layouts: 3.43 us -> 3.13 us
  transfers between devices with their start and end apart: 1 -> 0, of which waited for: 1 -> 0; matrix products, arithmetic and copies ran while one was open for 0% -> 0% of each run, Pallas kernels for 0% -> 0%
where the time goes in v1:
time: 68.8 us; the launch traced here: 68.6 us
  Pallas kernels  64.2 us (93%)
  local copies, waits for them, and re-layouts  3.13 us (5%)
    pallas_call x1, Pallas kernels, local_step(): pl.pallas_call(functools.partial(combine_kernel, n_tp, n_chunks), out_sha...  32 us
    pallas_call x1, Pallas kernels, local_step(): pl.pallas_call(functools.partial(attend_kernel, slots, heads), out_shape=...  16.1 us
    pallas_call x1, Pallas kernels, local_step(): pl.pallas_call(functools.partial(project_kernel, n_tp), out_shape=(by_hea...  16.1 us
    unnamed x1, local copies, waits for them, and re-layouts  3.13 us

profile of v1, /device:TPU:81, one launch (start us, length us, event | category | flops | bytes accessed | tf_op | source)
XLA Modules:
  0.0 68.6 jit_solution(3658661911234290590)
XLA Ops:
  0.6 0.6 maximum_bitcast_fusion.freq
  1.2 16.1 %project.1 = (bf16[4,256,128]{2,1,0:T(8,128)(2,1)}, bf16[4,256,128]{2,1,0:T(8,128)(2,1)}, bf16[4,256,128]{2,1,0:T(8,128)(2,1)}) custom-call(bf16[256,4096]{1,0:T(8,128)(2,1)} %hidden.3, bf16[4096,512]{1,0:T(8,128)(2,1)} %w_q.1, bf16[4096,512]{1,0:T(8,128)(2,1)} %w_k.1, bf16[4096,512]{1,0:T(8,128)(2,1)} %w_v.1, f32[1,512]{1,0:T(1,128)} %bitcast.15, ...), custom_call_target="tpu_custom_call" | custom-call | tf_op jit(solution)/shard_map/project/pallas_call | solution.py:379
  17.3 16.1 %attend.1 = (bf16[32768,128]{1,0:T(8,128)(2,1)}, bf16[32768,128]{1,0:T(8,128)(2,1)}, bf16[256,512]{1,0:T(8,128)(2,1)}) custom-call(s32[256]{0:T(256)} %pos_smem.1, s32[2,128]{1,0:T(2,128)} %bitcast.14, bf16[4,256,128]{2,1,0:T(8,128)(2,1)} %get-tuple-element.9.q, bf16[4,256,128]{2,1,0:T(8,128)(2,1)} %get-tuple-element.10.k, ...), custom_call_target="tpu_custom_call" | custom-call | tf_op jit(solution)/shard_map/attend/pallas_call | solution.py:403
  33.5 32.0 %combine.1 = bf16[256,4096]{1,0:T(8,128)(2,1)} custom-call(bf16[256,512]{1,0:T(8,128)(2,1)} %get-tuple-element.12.o, bf16[512,4096]{1,0:T(8,128)(2,1)} %w_o.1, bf16[256,4096]{1,0:T(8,128)(2,1)} %hidden.3, f32[1,4096]{1,0:T(1,128)} %bitcast.12), custom_call_target="tpu_custom_call" | custom-call | tf_op jit(solution)/shard_map/combine/pallas_call | solution.py:424
  65.5 3.1 %copy.15 = bf16[256,4096]{1,0:T(8,128)(2,1)} copy(bf16[256,4096]{1,0:T(8,128)(2,1)} %combine.1) | data formatting | bytes 4194304
  (1 shorter events, 0.0 us)
